TPU v7x, 32 devices: a whole 2x2x4 slice. The times are simulated.
32 devices in a mesh: dp: 8 (over z, x), section: 4 (over y, core).
Axes of the slice: x: 2, y: 2, z: 4, core: 2. Of those that a mesh axis runs over, the one named last changes fastest.
Arguments:
- entry_tokens: bfloat16 [8, 8, 16, 8192], P('dp'), may hold values from -6 to 6
- section_norm_gain: bfloat16 [4, 8192], P('section'), may hold values from 0.5 to 1.5
- adapter_down_weight: bfloat16 [4, 48, 8192], P('section'), may hold values from -0.0625 to 0.0625
- adapter_up_weight: bfloat16 [4, 48, 8192], P('section'), may hold values from -0.875 to 0.875
- output_gradient: bfloat16 [8, 8, 16, 8192], P('dp'), may hold values from -6 to 6
- lengths: int32 [8, 8], P('dp'), may hold values from 1 to 16
- keep: int32 [8, 4, 8, 16], P('dp', 'section'), may hold values from 0 to 1, as said below
Outputs:
- grad_up: float32 [4, 48, 8192], P('section')
- grad_gain: float32 [4, 8192], P('section')
Inputs may be any that keep to these rules, and one draw needn't show every extreme that they name: `keep`: 0 or 1; token 0 of every microbatch is kept at every section.
All inputs are finite; a program needn't handle non-finite values.
Results may differ from a plain program's by a relative error of at most 0.02.
Values may be sent and summed in bfloat16 or wider, within the bound.
No kernel may reach another device: no remote copies, remote signals or barrier semaphores. Data moves between devices by JAX's collectives and lax.ppermute only.
A program may use at most 64 MiB of HBM per device.

v0:
```python
import jax
import jax.numpy as jnp
from jax import lax
from jax.sharding import PartitionSpec as P

EPS = 1e-05


def passed_along(block, axis, distance):
    devices = range(lax.axis_size(axis))
    route = [(i - distance, i) for i in devices if i - distance in devices]
    return lax.ppermute(block, axis, route)


def section_apply(current_rows, gain_f32, down_rows, up_rows, weight):
    widened_rows = current_rows.astype(jnp.float32)
    inverse_norm = lax.rsqrt(jnp.mean(widened_rows * widened_rows, axis=-1, keepdims=True) + EPS)
    normed = (widened_rows * inverse_norm * gain_f32).astype(jnp.bfloat16)
    lowrank_rows = lax.dot_general(
        normed, down_rows, (((1,), (1,)), ((), ())), preferred_element_type=jnp.float32
    ).astype(jnp.bfloat16)
    branch = jnp.dot(lowrank_rows, up_rows, preferred_element_type=jnp.float32)
    section_output = (widened_rows + weight * branch).astype(jnp.bfloat16)
    row_energy = jnp.sum(weight * branch * branch, axis=1)
    return (section_output, lowrank_rows, row_energy)


def body(
    entry_tokens,
    section_norm_gain,
    adapter_down_weight,
    adapter_up_weight,
    output_gradient,
    lengths,
    keep,
):
    section_total = lax.axis_size("section")
    section_index = lax.axis_index("section")
    micro_count = entry_tokens.shape[1]
    token_count = entry_tokens.shape[2]
    model_width = entry_tokens.shape[3]
    rank_total = adapter_down_weight.shape[1]
    group_size = 2
    block_count = micro_count // group_size
    block_rows = group_size * token_count
    gain_f32 = section_norm_gain[0].astype(jnp.float32)
    down_rows = adapter_down_weight[0]
    up_rows = adapter_up_weight[0]
    position = jnp.arange(token_count, dtype=jnp.int32)
    valid_mask = (position[None, :] < lengths[0][:, None]).astype(jnp.float32)
    retained_mask = keep[0, 0].astype(jnp.float32) * valid_mask
    count_local = jnp.sum(retained_mask, axis=1)
    tick_count = block_count + section_total - 1
    block_ids = jnp.arange(block_count, dtype=jnp.int32)
    tokens_blocks = entry_tokens[0].reshape(block_count, block_rows, model_width)
    grad_blocks = output_gradient[0].reshape(block_count, block_rows, model_width)
    kept_blocks = retained_mask.reshape(block_count, block_rows)
    valid_blocks = valid_mask.reshape(block_count, block_rows)

    def forward_tick(step_index, state_tuple):
        incoming, stashed, low_stash, energy = state_tuple
        block_index = step_index - section_index
        active = (block_index >= 0) & (block_index < block_count)
        slot_index = jnp.clip(block_index, 0, block_count - 1)
        fresh_rows = lax.dynamic_index_in_dim(tokens_blocks, slot_index, 0, keepdims=False)
        current_rows = jnp.where(section_index == 0, fresh_rows, incoming)
        weight = lax.dynamic_index_in_dim(kept_blocks, slot_index, 0, keepdims=False)[:, None]
        section_output, lowrank_rows, row_energy = section_apply(
            current_rows, gain_f32, down_rows, up_rows, weight
        )
        block_energy = jnp.sum(row_energy.reshape(group_size, token_count), axis=1)
        old_rows = lax.dynamic_index_in_dim(stashed, slot_index, 0, keepdims=False)
        stashed = lax.dynamic_update_index_in_dim(
            stashed, jnp.where(active, current_rows, old_rows), slot_index, 0
        )
        old_low = lax.dynamic_index_in_dim(low_stash, slot_index, 0, keepdims=False)
        low_stash = lax.dynamic_update_index_in_dim(
            low_stash, jnp.where(active, lowrank_rows, old_low), slot_index, 0
        )
        energy = (
            energy + (block_ids == block_index).astype(jnp.float32)[:, None] * block_energy[None, :]
        )
        passed = passed_along(section_output, "section", 1)
        return (passed, stashed, low_stash, energy)

    start_state = (
        jnp.zeros((block_rows, model_width), jnp.bfloat16),
        jnp.zeros((block_count, block_rows, model_width), jnp.bfloat16),
        jnp.zeros((block_count, block_rows, rank_total), jnp.bfloat16),
        jnp.zeros((block_count, group_size), jnp.float32),
    )
    ignored, stashed, low_stash, energy_blocks = lax.fori_loop(
        0, tick_count, forward_tick, start_state
    )
    energy = energy_blocks.reshape(micro_count)
    total_energy, total_count = lax.psum((energy, count_local), "section")
    scaling = 1.0 / (total_count * jnp.sqrt(total_energy / (model_width * total_count) + EPS))
    scaling_rows = (scaling[:, None] * jnp.ones((1, token_count), jnp.float32)).reshape(
        block_count, block_rows
    )

    def backward_tick(step_index, state_tuple):
        incoming, grad_stash, gain_grad = state_tuple
        block_index = step_index - (section_total - 1 - section_index)
        active = (block_index >= 0) & (block_index < block_count)
        slot_index = jnp.clip(block_index, 0, block_count - 1)
        valid_row = lax.dynamic_index_in_dim(valid_blocks, slot_index, 0, keepdims=False)[:, None]
        scale_row = lax.dynamic_index_in_dim(scaling_rows, slot_index, 0, keepdims=False)[:, None]
        seed_rows = (
            lax.dynamic_index_in_dim(grad_blocks, slot_index, 0, keepdims=False).astype(jnp.float32)
            * valid_row
            * scale_row
        ).astype(jnp.bfloat16)
        cotangent = jnp.where(section_index == section_total - 1, seed_rows, incoming)
        current_rows = lax.dynamic_index_in_dim(stashed, slot_index, 0, keepdims=False)
        weight = lax.dynamic_index_in_dim(kept_blocks, slot_index, 0, keepdims=False)[:, None]
        widened_rows = current_rows.astype(jnp.float32)
        inverse_norm = lax.rsqrt(
            jnp.mean(widened_rows * widened_rows, axis=-1, keepdims=True) + EPS
        )
        branch_gradient = (weight * cotangent.astype(jnp.float32)).astype(jnp.bfloat16)
        lowrank_gradient = lax.dot_general(
            branch_gradient, up_rows, (((1,), (1,)), ((), ())), preferred_element_type=jnp.float32
        ).astype(jnp.bfloat16)
        norm_gradient = jnp.dot(lowrank_gradient, down_rows, preferred_element_type=jnp.float32)
        gain_grad = gain_grad + jnp.where(
            active, jnp.sum(norm_gradient * widened_rows * inverse_norm, axis=0), 0.0
        )
        scaled = norm_gradient * gain_f32
        input_grad = inverse_norm * scaled - widened_rows * inverse_norm**3 * jnp.mean(
            scaled * widened_rows, axis=-1, keepdims=True
        )
        updated = (cotangent.astype(jnp.float32) + input_grad).astype(jnp.bfloat16)
        old_rows = lax.dynamic_index_in_dim(grad_stash, slot_index, 0, keepdims=False)
        grad_stash = lax.dynamic_update_index_in_dim(
            grad_stash, jnp.where(active, branch_gradient, old_rows), slot_index, 0
        )
        passed = passed_along(updated, "section", -1)
        return (passed, grad_stash, gain_grad)

    back_state = (
        jnp.zeros((block_rows, model_width), jnp.bfloat16),
        jnp.zeros((block_count, block_rows, model_width), jnp.bfloat16),
        jnp.zeros((model_width,), jnp.float32),
    )
    ignored, grad_stash, gain_grad = lax.fori_loop(0, tick_count, backward_tick, back_state)
    low_rows = low_stash.reshape(micro_count * token_count, rank_total)
    grad_rows = grad_stash.reshape(micro_count * token_count, model_width)
    grad_section = lax.dot_general(
        low_rows, grad_rows, (((0,), (0,)), ((), ())), preferred_element_type=jnp.float32
    )
    summed_up, summed_gain = lax.psum((grad_section, gain_grad), "dp")
    return (summed_up[None], summed_gain[None])


def solution(mesh):
    in_specs = (
        P("dp", None, None, None),
        P("section", None),
        P("section", None, None),
        P("section", None, None),
        P("dp", None, None, None),
        P("dp", None),
        P("dp", "section", None, None),
    )
    out_specs = (P("section", None, None), P("section", None))
    return jax.shard_map(body, mesh=mesh, in_specs=in_specs, out_specs=out_specs, check_vma=False)
```

profile of v0, /device:TPU:0, one launch (start us, length us, event | category | flops | bytes accessed | tf_op | source)
XLA Modules:
  0.0 365.9 jit_solution(720218584703908973)
XLA Ops:
  13.5 97.0 %while.41 = (s32[]{:T(128)}, bf16[32,8192]{1,0:T(8,128)(2,1)S(1)}, bf16[4,32,8192]{2,1,0:T(8,128)(2,1)}, bf16[4,32,48]{2,1,0:T(8,128)(2,1)S(1)}, f32[4,2]{0,1:T(...) while((s32[]{:T(128)}, bf16[32,8192]{1,0:T(8,128)(2,1)S(1)}, ...), condition=%wide.region_4.5_spmd.clone, body=%wide.region_0.4_spmd.clone.sunk | while | flops 54266952 | bytes 9506454 | solution.py:92
  17.8 2.4 collective-permute-start
  26.0 9.1 %collective-permute-start = (bf16[32,8192]{1,0:T(8,128)(2,1)S(1)}, bf16[32,8192]{1,0:T(8,128)(2,1)S(1)}, u32[]{:S(2)}, u32[]{:S(2)}) collective-permute-start(bf16[32,8192]{1,0:T(8,128)(2,1)S(1)} %get-tuple-element.881), channel_id=1, source_target_pairs={{0,1},{1,2},{2,3},{4,5},{5,6},{6,7},{8,9},{9,10},{10,11},{12,13},{... | collective-permute-start | bytes 1572872 | tf_op jit(solution)/shard_map/while/body/eval_jaxpr/ppermute | solution.py:12
  40.8 9.0 %collective-permute-start = (bf16[32,8192]{1,0:T(8,128)(2,1)S(1)}, bf16[32,8192]{1,0:T(8,128)(2,1)S(1)}, u32[]{:S(2)}, u32[]{:S(2)}) collective-permute-start(bf16[32,8192]{1,0:T(8,128)(2,1)S(1)} %get-tuple-element.881), channel_id=1, source_target_pairs={{0,1},{1,2},{2,3},{4,5},{5,6},{6,7},{8,9},{9,10},{10,11},{12,13},{... | collective-permute-start | bytes 1572872 | tf_op jit(solution)/shard_map/while/body/eval_jaxpr/ppermute | solution.py:12
  55.7 9.0 %collective-permute-start = (bf16[32,8192]{1,0:T(8,128)(2,1)S(1)}, bf16[32,8192]{1,0:T(8,128)(2,1)S(1)}, u32[]{:S(2)}, u32[]{:S(2)}) collective-permute-start(bf16[32,8192]{1,0:T(8,128)(2,1)S(1)} %get-tuple-element.881), channel_id=1, source_target_pairs={{0,1},{1,2},{2,3},{4,5},{5,6},{6,7},{8,9},{9,10},{10,11},{12,13},{... | collective-permute-start | bytes 1572872 | tf_op jit(solution)/shard_map/while/body/eval_jaxpr/ppermute | solution.py:12
  70.4 9.0 %collective-permute-start = (bf16[32,8192]{1,0:T(8,128)(2,1)S(1)}, bf16[32,8192]{1,0:T(8,128)(2,1)S(1)}, u32[]{:S(2)}, u32[]{:S(2)}) collective-permute-start(bf16[32,8192]{1,0:T(8,128)(2,1)S(1)} %get-tuple-element.881), channel_id=1, source_target_pairs={{0,1},{1,2},{2,3},{4,5},{5,6},{6,7},{8,9},{9,10},{10,11},{12,13},{... | collective-permute-start | bytes 1572872 | tf_op jit(solution)/shard_map/while/body/eval_jaxpr/ppermute | solution.py:12
  85.2 9.0 %collective-permute-start = (bf16[32,8192]{1,0:T(8,128)(2,1)S(1)}, bf16[32,8192]{1,0:T(8,128)(2,1)S(1)}, u32[]{:S(2)}, u32[]{:S(2)}) collective-permute-start(bf16[32,8192]{1,0:T(8,128)(2,1)S(1)} %get-tuple-element.881), channel_id=1, source_target_pairs={{0,1},{1,2},{2,3},{4,5},{5,6},{6,7},{8,9},{9,10},{10,11},{12,13},{... | collective-permute-start | bytes 1572872 | tf_op jit(solution)/shard_map/while/body/eval_jaxpr/ppermute | solution.py:12
  100.0 9.0 %collective-permute-start = (bf16[32,8192]{1,0:T(8,128)(2,1)S(1)}, bf16[32,8192]{1,0:T(8,128)(2,1)S(1)}, u32[]{:S(2)}, u32[]{:S(2)}) collective-permute-start(bf16[32,8192]{1,0:T(8,128)(2,1)S(1)} %get-tuple-element.881), channel_id=1, source_target_pairs={{0,1},{1,2},{2,3},{4,5},{5,6},{6,7},{8,9},{9,10},{10,11},{12,13},{... | collective-permute-start | bytes 1572872 | tf_op jit(solution)/shard_map/while/body/eval_jaxpr/ppermute | solution.py:12
  110.6 13.0 %all-reduce = (f32[8]{0:T(128)S(1)}, f32[8]{0:T(128)S(1)}) all-reduce(f32[8]{0:T(128)S(1)} %fusion.28, f32[8]{0:T(128)S(1)} %reshape.98), channel_id=1, replica_groups=mesh['dp'=8,'section'=4] {'section'}, use_global_device_ids=true, to_apply=%region_6.7 | all-reduce | flops 16 | bytes 128 | tf_op jit(solution)/shard_map/psum | solution.py:96
  125.5 130.7 %while.42 = (s32[]{:T(128)}, bf16[32,8192]{1,0:T(8,128)(2,1)S(1)}, bf16[4,32,8192]{2,1,0:T(8,128)(2,1)}, f32[8192]{0:T(1024)S(1)}, pred[]{:T(512)}, /*index=5*/s...) while((s32[]{:T(128)}, bf16[32,8192]{1,0:T(8,128)(2,1)S(1)}, ...), condition=%wide.region_12.13_spmd.clone, body=%wide.region_8.12_spmd.clone.sunk | while | flops 58476136 | bytes 12783022 | solution.py:146
  127.9 2.2 bitcast_dynamic-update-slice_fusion.8
  132.2 2.2 fusion.67
  135.7 2.7 collective-permute-done.1
  140.8 2.2 bitcast_dynamic-update-slice_fusion.8
  145.1 2.2 fusion.67
  148.6 9.5 %collective-permute-done.1 = bf16[32,8192]{1,0:T(8,128)(2,1)S(1)} collective-permute-done((bf16[32,8192]{1,0:T(8,128)(2,1)}, bf16[32,8192]{1,0:T(8,128)(2,1)S(1)}, u32[]{:S(2)}, u32[]{:S(2)}) %collective-permute-start.1) | collective-permute-done | bytes 524320 | tf_op jit(solution)/shard_map/while/body/eval_jaxpr/ppermute | solution.py:12
  160.5 2.2 bitcast_dynamic-update-slice_fusion.8
  164.8 2.2 fusion.67
  168.3 9.4 %collective-permute-done.1 = bf16[32,8192]{1,0:T(8,128)(2,1)S(1)} collective-permute-done((bf16[32,8192]{1,0:T(8,128)(2,1)}, bf16[32,8192]{1,0:T(8,128)(2,1)S(1)}, u32[]{:S(2)}, u32[]{:S(2)}) %collective-permute-start.1) | collective-permute-done | bytes 524320 | tf_op jit(solution)/shard_map/while/body/eval_jaxpr/ppermute | solution.py:12
  180.1 2.2 bitcast_dynamic-update-slice_fusion.8
  187.9 9.4 %collective-permute-done.1 = bf16[32,8192]{1,0:T(8,128)(2,1)S(1)} collective-permute-done((bf16[32,8192]{1,0:T(8,128)(2,1)}, bf16[32,8192]{1,0:T(8,128)(2,1)S(1)}, u32[]{:S(2)}, u32[]{:S(2)}) %collective-permute-start.1) | collective-permute-done | bytes 524320 | tf_op jit(solution)/shard_map/while/body/eval_jaxpr/ppermute | solution.py:12
  199.7 2.2 bitcast_dynamic-update-slice_fusion.8
  204.1 2.2 fusion.67
  207.6 9.4 %collective-permute-done.1 = bf16[32,8192]{1,0:T(8,128)(2,1)S(1)} collective-permute-done((bf16[32,8192]{1,0:T(8,128)(2,1)}, bf16[32,8192]{1,0:T(8,128)(2,1)S(1)}, u32[]{:S(2)}, u32[]{:S(2)}) %collective-permute-start.1) | collective-permute-done | bytes 524320 | tf_op jit(solution)/shard_map/while/body/eval_jaxpr/ppermute | solution.py:12
  219.3 2.2 bitcast_dynamic-update-slice_fusion.8
  227.2 9.4 %collective-permute-done.1 = bf16[32,8192]{1,0:T(8,128)(2,1)S(1)} collective-permute-done((bf16[32,8192]{1,0:T(8,128)(2,1)}, bf16[32,8192]{1,0:T(8,128)(2,1)S(1)}, u32[]{:S(2)}, u32[]{:S(2)}) %collective-permute-start.1) | collective-permute-done | bytes 524320 | tf_op jit(solution)/shard_map/while/body/eval_jaxpr/ppermute | solution.py:12
  238.9 2.2 bitcast_dynamic-update-slice_fusion.8
  246.8 9.4 %collective-permute-done.1 = bf16[32,8192]{1,0:T(8,128)(2,1)S(1)} collective-permute-done((bf16[32,8192]{1,0:T(8,128)(2,1)}, bf16[32,8192]{1,0:T(8,128)(2,1)S(1)}, u32[]{:S(2)}, u32[]{:S(2)}) %collective-permute-start.1) | collective-permute-done | bytes 524320 | tf_op jit(solution)/shard_map/while/body/eval_jaxpr/ppermute | solution.py:12
  256.2 3.2 convolution_bitcast_fusion
  259.4 38.7 %psum.31 = f32[1,8192]{1,0:T(1,128)} all-reduce(f32[1,8192]{1,0:T(1,128)S(1)} %bitcast.101), channel_id=1, replica_groups=mesh['dp'=8,'section'=4] {'dp'}, use_global_device_ids=true, to_apply=%region_14.15 | all-reduce | flops 8192 | bytes 65536 | tf_op jit(solution)/shard_map/psum | solution.py:152
  298.1 58.2 %all-reduce.3.cloned.1.call-done = f32[1,48,8192]{2,1,0:T(8,128)} async-done(((f32[1,48,8192]{2,1,0:T(8,128)}), f32[1,48,8192]{2,1,0:T(8,128)}) %all-reduce.3.cloned.1.call-update) | async-done | bytes 1572880 | tf_op jit(solution)/shard_map/psum | solution.py:152
  356.4 2.7 copy.42
  (189 shorter events, 95.4 us)
Async XLA Ops:
  7.2 6.3 %copy-start = (bf16[1,48,8192]{2,1,0:T(8,128)(2,1)S(1)}, bf16[1,48,8192]{2,1,0:T(8,128)(2,1)}, u32[]{:S(2)}) copy-start(bf16[1,48,8192]{2,1,0:T(8,128)(2,1)} %param.14) | copy-start | bytes 2359300
  7.2 6.3 %copy-start.1 = (bf16[1,48,8192]{2,1,0:T(8,128)(2,1)S(1)}, bf16[1,48,8192]{2,1,0:T(8,128)(2,1)}, u32[]{:S(2)}) copy-start(bf16[1,48,8192]{2,1,0:T(8,128)(2,1)} %param.13) | copy-start | bytes 2359300
  7.2 349.2 %all-reduce.3.cloned.1.call-start = ((), (), s32[]{:S(2)}) async-start(), calls=%async_computation | async-start | bytes 3145728 | tf_op jit(solution)/shard_map/psum | solution.py:152
  17.8 3.9 %collective-permute-start = (bf16[32,8192]{1,0:T(8,128)(2,1)S(1)}, bf16[32,8192]{1,0:T(8,128)(2,1)S(1)}, u32[]{:S(2)}, u32[]{:S(2)}) collective-permute-start(bf16[32,8192]{1,0:T(8,128)(2,1)S(1)} %get-tuple-element.881), channel_id=1, source_target_pairs={{0,1},{1,2},{2,3},{4,5},{5,6},{6,7},{8,9},{9,10},{10,11},{12,13},{... | collective-permute-start | bytes 1572872 | tf_op jit(solution)/shard_map/while/body/eval_jaxpr/ppermute | solution.py:12
  26.0 10.6 %collective-permute-start = (bf16[32,8192]{1,0:T(8,128)(2,1)S(1)}, bf16[32,8192]{1,0:T(8,128)(2,1)S(1)}, u32[]{:S(2)}, u32[]{:S(2)}) collective-permute-start(bf16[32,8192]{1,0:T(8,128)(2,1)S(1)} %get-tuple-element.881), channel_id=1, source_target_pairs={{0,1},{1,2},{2,3},{4,5},{5,6},{6,7},{8,9},{9,10},{10,11},{12,13},{... | collective-permute-start | bytes 1572872 | tf_op jit(solution)/shard_map/while/body/eval_jaxpr/ppermute | solution.py:12
  40.8 10.5 %collective-permute-start = (bf16[32,8192]{1,0:T(8,128)(2,1)S(1)}, bf16[32,8192]{1,0:T(8,128)(2,1)S(1)}, u32[]{:S(2)}, u32[]{:S(2)}) collective-permute-start(bf16[32,8192]{1,0:T(8,128)(2,1)S(1)} %get-tuple-element.881), channel_id=1, source_target_pairs={{0,1},{1,2},{2,3},{4,5},{5,6},{6,7},{8,9},{9,10},{10,11},{12,13},{... | collective-permute-start | bytes 1572872 | tf_op jit(solution)/shard_map/while/body/eval_jaxpr/ppermute | solution.py:12
  55.7 10.5 %collective-permute-start = (bf16[32,8192]{1,0:T(8,128)(2,1)S(1)}, bf16[32,8192]{1,0:T(8,128)(2,1)S(1)}, u32[]{:S(2)}, u32[]{:S(2)}) collective-permute-start(bf16[32,8192]{1,0:T(8,128)(2,1)S(1)} %get-tuple-element.881), channel_id=1, source_target_pairs={{0,1},{1,2},{2,3},{4,5},{5,6},{6,7},{8,9},{9,10},{10,11},{12,13},{... | collective-permute-start | bytes 1572872 | tf_op jit(solution)/shard_map/while/body/eval_jaxpr/ppermute | solution.py:12
  70.4 10.5 %collective-permute-start = (bf16[32,8192]{1,0:T(8,128)(2,1)S(1)}, bf16[32,8192]{1,0:T(8,128)(2,1)S(1)}, u32[]{:S(2)}, u32[]{:S(2)}) collective-permute-start(bf16[32,8192]{1,0:T(8,128)(2,1)S(1)} %get-tuple-element.881), channel_id=1, source_target_pairs={{0,1},{1,2},{2,3},{4,5},{5,6},{6,7},{8,9},{9,10},{10,11},{12,13},{... | collective-permute-start | bytes 1572872 | tf_op jit(solution)/shard_map/while/body/eval_jaxpr/ppermute | solution.py:12
  85.2 10.5 %collective-permute-start = (bf16[32,8192]{1,0:T(8,128)(2,1)S(1)}, bf16[32,8192]{1,0:T(8,128)(2,1)S(1)}, u32[]{:S(2)}, u32[]{:S(2)}) collective-permute-start(bf16[32,8192]{1,0:T(8,128)(2,1)S(1)} %get-tuple-element.881), channel_id=1, source_target_pairs={{0,1},{1,2},{2,3},{4,5},{5,6},{6,7},{8,9},{9,10},{10,11},{12,13},{... | collective-permute-start | bytes 1572872 | tf_op jit(solution)/shard_map/while/body/eval_jaxpr/ppermute | solution.py:12
  100.0 10.5 %collective-permute-start = (bf16[32,8192]{1,0:T(8,128)(2,1)S(1)}, bf16[32,8192]{1,0:T(8,128)(2,1)S(1)}, u32[]{:S(2)}, u32[]{:S(2)}) collective-permute-start(bf16[32,8192]{1,0:T(8,128)(2,1)S(1)} %get-tuple-element.881), channel_id=1, source_target_pairs={{0,1},{1,2},{2,3},{4,5},{5,6},{6,7},{8,9},{9,10},{10,11},{12,13},{... | collective-permute-start | bytes 1572872 | tf_op jit(solution)/shard_map/while/body/eval_jaxpr/ppermute | solution.py:12
  134.4 4.0 %collective-permute-start.1 = (bf16[32,8192]{1,0:T(8,128)(2,1)}, bf16[32,8192]{1,0:T(8,128)(2,1)S(1)}, u32[]{:S(2)}, u32[]{:S(2)}) collective-permute-start(bf16[32,8192]{1,0:T(8,128)(2,1)} %fusion.67), channel_id=1, source_target_pairs={{1,0},{2,1},{3,2},{5,4},{6,5},{7,6},{9,8},{10,9},{11,10},{13,12},{... | collective-permute-start | bytes 1572872 | tf_op jit(solution)/shard_map/while/body/eval_jaxpr/ppermute | solution.py:12
  147.3 10.8 %collective-permute-start.1 = (bf16[32,8192]{1,0:T(8,128)(2,1)}, bf16[32,8192]{1,0:T(8,128)(2,1)S(1)}, u32[]{:S(2)}, u32[]{:S(2)}) collective-permute-start(bf16[32,8192]{1,0:T(8,128)(2,1)} %fusion.67), channel_id=1, source_target_pairs={{1,0},{2,1},{3,2},{5,4},{6,5},{7,6},{9,8},{10,9},{11,10},{13,12},{... | collective-permute-start | bytes 1572872 | tf_op jit(solution)/shard_map/while/body/eval_jaxpr/ppermute | solution.py:12
  167.0 10.7 %collective-permute-start.1 = (bf16[32,8192]{1,0:T(8,128)(2,1)}, bf16[32,8192]{1,0:T(8,128)(2,1)S(1)}, u32[]{:S(2)}, u32[]{:S(2)}) collective-permute-start(bf16[32,8192]{1,0:T(8,128)(2,1)} %fusion.67), channel_id=1, source_target_pairs={{1,0},{2,1},{3,2},{5,4},{6,5},{7,6},{9,8},{10,9},{11,10},{13,12},{... | collective-permute-start | bytes 1572872 | tf_op jit(solution)/shard_map/while/body/eval_jaxpr/ppermute | solution.py:12
  186.6 10.7 %collective-permute-start.1 = (bf16[32,8192]{1,0:T(8,128)(2,1)}, bf16[32,8192]{1,0:T(8,128)(2,1)S(1)}, u32[]{:S(2)}, u32[]{:S(2)}) collective-permute-start(bf16[32,8192]{1,0:T(8,128)(2,1)} %fusion.67), channel_id=1, source_target_pairs={{1,0},{2,1},{3,2},{5,4},{6,5},{7,6},{9,8},{10,9},{11,10},{13,12},{... | collective-permute-start | bytes 1572872 | tf_op jit(solution)/shard_map/while/body/eval_jaxpr/ppermute | solution.py:12
  206.2 10.7 %collective-permute-start.1 = (bf16[32,8192]{1,0:T(8,128)(2,1)}, bf16[32,8192]{1,0:T(8,128)(2,1)S(1)}, u32[]{:S(2)}, u32[]{:S(2)}) collective-permute-start(bf16[32,8192]{1,0:T(8,128)(2,1)} %fusion.67), channel_id=1, source_target_pairs={{1,0},{2,1},{3,2},{5,4},{6,5},{7,6},{9,8},{10,9},{11,10},{13,12},{... | collective-permute-start | bytes 1572872 | tf_op jit(solution)/shard_map/while/body/eval_jaxpr/ppermute | solution.py:12
  225.9 10.7 %collective-permute-start.1 = (bf16[32,8192]{1,0:T(8,128)(2,1)}, bf16[32,8192]{1,0:T(8,128)(2,1)S(1)}, u32[]{:S(2)}, u32[]{:S(2)}) collective-permute-start(bf16[32,8192]{1,0:T(8,128)(2,1)} %fusion.67), channel_id=1, source_target_pairs={{1,0},{2,1},{3,2},{5,4},{6,5},{7,6},{9,8},{10,9},{11,10},{13,12},{... | collective-permute-start | bytes 1572872 | tf_op jit(solution)/shard_map/while/body/eval_jaxpr/ppermute | solution.py:12
  245.5 10.7 %collective-permute-start.1 = (bf16[32,8192]{1,0:T(8,128)(2,1)}, bf16[32,8192]{1,0:T(8,128)(2,1)S(1)}, u32[]{:S(2)}, u32[]{:S(2)}) collective-permute-start(bf16[32,8192]{1,0:T(8,128)(2,1)} %fusion.67), channel_id=1, source_target_pairs={{1,0},{2,1},{3,2},{5,4},{6,5},{7,6},{9,8},{10,9},{11,10},{13,12},{... | collective-permute-start | bytes 1572872 | tf_op jit(solution)/shard_map/while/body/eval_jaxpr/ppermute | solution.py:12
Sparse Core Ops, SparseCore 0:
  259.5 96.7 all-reduce.2
where the time goes:
time: 369 us; the launch traced here: 366 us
  waiting for transfers between devices  126 us (34%)
  starting transfers between devices  65.6 us (18%)
  other arithmetic  61.1 us (17%)
  blocking collectives  51.7 us (14%)
  matrix products  24 us (7%)
  local copies, waits for them, and re-layouts  23 us (6%)
  between operations  14.1 us (4%)
    ppermute x14, waiting for transfers between devices, passed_along(): return lax.ppermute(block, axis, route)  67.5 us
    ppermute x14, starting transfers between devices, passed_along(): return lax.ppermute(block, axis, route)  65.5 us
    psum x1, waiting for transfers between devices, body(): summed_up, summed_gain = lax.psum((grad_section, gain_grad), 'dp')  58.2 us
    psum x1, blocking collectives, body(): summed_up, summed_gain = lax.psum((grad_section, gain_grad), 'dp')  38.7 us
    dynamic_update_slice x7, other arithmetic, backward_tick(): lax.dynamic_update_index_in_dim(grad_stash, jnp.where(active, branch_grad...  15.5 us
    convert_element_type x7, other arithmetic, backward_tick(): updated = (cotangent.astype(jnp.float32) + input_grad).astype(jnp.bfloat16)  15.3 us
    dot_general x7, matrix products, backward_tick(): jnp.dot(lowrank_gradient, down_rows, preferred_element_type=jnp.float32)  14.8 us
    dynamic_update_slice x7, other arithmetic, forward_tick(): lax.dynamic_update_index_in_dim(stashed, jnp.where(active, current_rows,...  14.5 us
  transfers between devices with their start and end apart: 15, of which 15 were waited for; matrix products, arithmetic and copies ran while one was open for 1% of the time, Pallas kernels for 0%

commit v1 on v0

--- a/solution.py
+++ b/solution.py
@@ -1,6 +1,8 @@
 import jax
 import jax.numpy as jnp
 from jax import lax
+from jax.experimental import pallas as pl
+from jax.experimental.pallas import tpu as pltpu
 from jax.sharding import PartitionSpec as P
 
 EPS = 1e-05
@@ -25,7 +27,7 @@
     return (section_output, lowrank_rows, row_energy)
 
 
-def body(
+def relay_body(
     entry_tokens,
     section_norm_gain,
     adapter_down_weight,
@@ -153,6 +155,345 @@
     return (summed_up[None], summed_gain[None])
 
 
+LANES = 128
+PIECES = 4
+VMEM_BUDGET = 56 * 1024 * 1024
+
+
+def swapped(block, axis, bit):
+    route = [(i, i ^ bit) for i in range(lax.axis_size(axis))]
+    return lax.ppermute(block, axis, route)
+
+
+def rank_space_kernel(
+    index_ref, masks_ref, tokens_hbm, grads_hbm, *rest, sections, rank, width, micro, tokens, parts
+):
+    weights_hbm = rest[:sections]
+    down_hbm, payload_ref, stack, down, gram, proj, branch_stash, turned, sems = rest[sections:]
+    rows = micro * tokens
+    span = stack.shape[0] - 2 * rows
+    half = span // 2
+    model_width = stack.shape[1]
+    piece = model_width // PIECES
+    own = index_ref[0]
+    copies = []
+    for p in range(PIECES):
+        columns = pl.ds(p * piece, piece)
+        group = [
+            pltpu.make_async_copy(
+                tokens_hbm.at[:, columns], stack.at[pl.ds(span, rows), columns], sems.at[p, 0]
+            ),
+            pltpu.make_async_copy(
+                grads_hbm.at[:, columns], stack.at[pl.ds(span + rows, rows), columns], sems.at[p, 1]
+            ),
+        ]
+        for k in range(sections):
+            start = pl.multiple_of((own ^ k) * rank, 16)
+            for q in range(2):
+                group.append(
+                    pltpu.make_async_copy(
+                        weights_hbm[k].at[pl.ds(q * rank, rank), columns],
+                        stack.at[pl.ds(q * half + start, rank), columns],
+                        sems.at[p, 2 + 2 * k + q],
+                    )
+                )
+        for copy in group:
+            copy.start()
+        copies.append(group)
+    down_copy = pltpu.make_async_copy(down_hbm, down, sems.at[0, 2 + 2 * sections])
+    down_copy.start()
+    used = sections * rank
+    for q in range(2):
+        if used < half:
+            stack[q * half + used : (q + 1) * half, :] = jnp.zeros(
+                (half - used, model_width), jnp.bfloat16
+            )
+    square = jnp.zeros((rows, LANES), jnp.float32)
+    for p in range(PIECES):
+        for copy in copies[p]:
+            copy.wait()
+        columns = slice(p * piece, (p + 1) * piece)
+        product = lax.dot_general(
+            stack[half:, columns],
+            stack[:span, columns],
+            (((1,), (1,)), ((), ())),
+            preferred_element_type=jnp.float32,
+        )
+        if p == 0:
+            gram[...] = product[:half]
+            proj[...] = product[half:]
+        else:
+            gram[...] += product[:half]
+            proj[...] += product[half:]
+        for j in range(piece // LANES):
+            lane = p * piece + j * LANES
+            values = stack[span : span + rows, lane : lane + LANES].astype(jnp.float32)
+            square += values * values
+    norm_sq = jnp.sum(square, axis=1, keepdims=True)
+
+    lane_ids = lax.broadcasted_iota(jnp.int32, (rows, half), 1)
+    blocks = [(lane_ids >= s * rank) & (lane_ids < (s + 1) * rank) for s in range(sections)]
+    kept = [masks_ref[:, s : s + 1] for s in range(sections)]
+    valid = masks_ref[:, sections : sections + 1]
+    gram_hi = gram[...].astype(jnp.bfloat16)
+    gram_lo = (gram[...] - gram_hi.astype(jnp.float32)).astype(jnp.bfloat16)
+    down_side = proj[:rows, :half]
+    up_side = proj[:rows, half:]
+    down_saved = jnp.zeros((rows, half), jnp.float32)
+    kept_low = jnp.zeros((rows, half), jnp.float32)
+    power = jnp.zeros((rows, 1), jnp.float32)
+    count = jnp.zeros((rows, 1), jnp.float32)
+    inverses = []
+    for s in range(sections):
+        inverse = lax.rsqrt(norm_sq / width + EPS)
+        inverses.append(inverse)
+        masked = jnp.where(blocks[s], down_side, 0.0)
+        down_saved += masked
+        low = (masked * inverse).astype(jnp.bfloat16)
+        low_f32 = low.astype(jnp.float32)
+        kept_low += kept[s] * low_f32
+        branch_stash[s] = up_side
+        moved = jnp.dot(low, gram_hi, preferred_element_type=jnp.float32) + jnp.dot(
+            low, gram_lo, preferred_element_type=jnp.float32
+        )
+        energy = jnp.sum(low_f32 * moved[:, half:], axis=1, keepdims=True)
+        cross = jnp.sum(low_f32 * up_side, axis=1, keepdims=True)
+        power += kept[s] * energy
+        count += kept[s]
+        norm_sq = jnp.maximum(norm_sq + kept[s] * (2.0 * cross + energy), 0.0)
+        down_side = down_side + kept[s] * moved[:, :half]
+        up_side = up_side + kept[s] * moved[:, half:]
+
+    def per_micro(column):
+        wide = jnp.broadcast_to(column, (rows, LANES)).reshape(micro, tokens, LANES)
+        total = jnp.broadcast_to(jnp.sum(wide, axis=1, keepdims=True), wide.shape)
+        return total.reshape(rows, LANES)[:, :1]
+
+    total_energy = jnp.maximum(per_micro(power), 0.0)
+    total_count = per_micro(count)
+    scaling = 1.0 / (total_count * jnp.sqrt(total_energy / (width * total_count) + EPS))
+    alpha = valid * scaling
+
+    carried = alpha * proj[rows:, half:]
+    scaled_grad = jnp.zeros((rows, half), jnp.float32)
+    later = jnp.zeros((rows, half), jnp.float32)
+    weights = [None] * sections
+    zero = jnp.zeros((rows, 1), jnp.float32)
+    beta = zero
+    for s in reversed(range(sections)):
+        lowgrad = jnp.where(blocks[s], kept[s] * carried, 0.0).astype(jnp.bfloat16)
+        lowgrad_f32 = lowgrad.astype(jnp.float32)
+        mean = jnp.sum(lowgrad_f32 * down_saved, axis=1, keepdims=True) / width
+        inverse = inverses[s]
+        pull = inverse * inverse * inverse * mean
+        weights[s] = pull
+        scaled = inverse * lowgrad_f32
+        scaled_grad += scaled
+        if s > 0:
+            back = lax.dot_general(
+                lowgrad, gram_hi[:, :half], (((1,), (1,)), ((), ())), preferred_element_type=jnp.float32
+            ) + lax.dot_general(
+                lowgrad, gram_lo[:, :half], (((1,), (1,)), ((), ())), preferred_element_type=jnp.float32
+            )
+            carried = carried + inverse * back - pull * branch_stash[s]
+
+    beta = zero
+    gamma = jnp.zeros((rows, half), jnp.float32)
+    for s in reversed(range(sections)):
+        gamma = jnp.where(blocks[s], beta, gamma)
+        beta = beta + jnp.where(s > own, weights[s], zero)
+    low_edge = own * rank
+    high_edge = low_edge + rank
+    after = jnp.where(lane_ids >= high_edge, scaled_grad, 0.0).astype(jnp.bfloat16)
+    before = jnp.where(lane_ids < low_edge, kept_low, 0.0).astype(jnp.bfloat16)
+    pulled = (gamma * kept_low).astype(jnp.bfloat16)
+    turned[0] = (alpha * kept_low).T
+    turned[1] = (-beta * kept_low).T
+    turned[2] = kept_low.T
+    turned[3] = scaled_grad.T
+    mine = pl.ds(pl.multiple_of(low_edge, 16), rank)
+    low_own = turned[2, mine, :].astype(jnp.bfloat16)
+    grad_own = turned[3, mine, :].astype(jnp.bfloat16)
+    coef_up = [
+        turned[1, mine, :].astype(jnp.bfloat16),
+        turned[0, mine, :].astype(jnp.bfloat16),
+        jnp.dot(low_own, after, preferred_element_type=jnp.float32).astype(jnp.bfloat16),
+        -jnp.dot(low_own, pulled, preferred_element_type=jnp.float32).astype(jnp.bfloat16),
+    ]
+    coef_gain = [
+        grad_own,
+        jnp.dot(grad_own, before, preferred_element_type=jnp.float32).astype(jnp.bfloat16),
+    ]
+    left = jnp.concatenate(
+        [
+            jnp.concatenate([coef_up[2], coef_up[3], coef_up[0], coef_up[1]], axis=1),
+            jnp.concatenate(
+                [
+                    jnp.zeros((rank, half), jnp.bfloat16),
+                    coef_gain[1],
+                    coef_gain[0],
+                    jnp.zeros((rank, rows), jnp.bfloat16),
+                ],
+                axis=1,
+            ),
+        ],
+        axis=0,
+    )
+    down_copy.wait()
+    chunk = model_width // parts
+    lane_blocks = chunk // LANES
+    tail = payload_ref.shape[1] - lane_blocks * rank
+    for c in range(parts):
+        columns = slice(c * chunk, (c + 1) * chunk)
+        result = jnp.dot(left, stack[:, columns], preferred_element_type=jnp.float32)
+        gain = jnp.sum(
+            result[rank:] * down[:, columns].astype(jnp.float32), axis=0, keepdims=True
+        )
+        for j in range(lane_blocks):
+            payload_ref[c, j * rank : (j + 1) * rank, :] = result[
+                :rank, j * LANES : (j + 1) * LANES
+            ].astype(jnp.bfloat16)
+        gain_rows = [gain[:, j * LANES : (j + 1) * LANES] for j in range(lane_blocks)]
+        gain_rows.append(jnp.zeros((tail - lane_blocks, LANES), jnp.float32))
+        payload_ref[c, lane_blocks * rank :, :] = jnp.concatenate(gain_rows, axis=0).astype(
+            jnp.bfloat16
+        )
+
+
+def sum_kernel(parts_ref, out_ref):
+    total = parts_ref[0].astype(jnp.float32)
+    for c in range(1, parts_ref.shape[0]):
+        total += parts_ref[c].astype(jnp.float32)
+    rounded = total.astype(jnp.bfloat16)
+    for c in range(out_ref.shape[0]):
+        out_ref[c] = rounded
+
+
+def unpack_kernel(parts_ref, up_ref, gain_ref):
+    parts = parts_ref.shape[0]
+    rank = up_ref.shape[0]
+    chunk = up_ref.shape[1] // parts
+    lane_blocks = chunk // LANES
+    for c in range(parts):
+        tail = parts_ref[c, lane_blocks * rank :, :].astype(jnp.float32)
+        for j in range(lane_blocks):
+            lanes = slice(c * chunk + j * LANES, c * chunk + (j + 1) * LANES)
+            up_ref[:, lanes] = parts_ref[c, j * rank : (j + 1) * rank, :].astype(jnp.float32)
+            gain_ref[:, lanes] = tail[j : j + 1, :]
+
+
+def rank_space_body(
+    entry_tokens,
+    section_norm_gain,
+    adapter_down_weight,
+    adapter_up_weight,
+    output_gradient,
+    lengths,
+    keep,
+):
+    sections = lax.axis_size("section")
+    parts = lax.axis_size("dp")
+    section_index = lax.axis_index("section")
+    micro, tokens, width = entry_tokens.shape[1:]
+    rank = adapter_down_weight.shape[1]
+    rows = micro * tokens
+    down = adapter_down_weight[0]
+    scaled_down = (
+        section_norm_gain[0].astype(jnp.float32) * down.astype(jnp.float32)
+    ).astype(jnp.bfloat16)
+    weights = [jnp.concatenate([scaled_down, adapter_up_weight[0]], axis=0)]
+    bit = 1
+    while bit < sections:
+        fresh = swapped(weights[0], "section", bit)
+        more = [fresh]
+        for k in range(1, bit):
+            more.append(swapped(fresh, "section", k))
+        weights = weights + more
+        bit *= 2
+    valid = (jnp.arange(tokens, dtype=jnp.int32)[None, :] < lengths[0][:, None]).astype(jnp.float32)
+    kept_all = lax.all_gather(keep[0, 0], "section").astype(jnp.float32) * valid[None]
+    masks = jnp.concatenate([kept_all.reshape(sections, rows), valid.reshape(1, rows)], axis=0).T
+    half = -(-sections * rank // LANES) * LANES
+    lane_blocks = width // parts // LANES
+    payload_rows = lane_blocks * rank + -(-lane_blocks // 16) * 16
+    hbm = pl.BlockSpec(memory_space=pltpu.MemorySpace.HBM)
+    vmem = pl.BlockSpec(memory_space=pltpu.MemorySpace.VMEM)
+    payload = pl.pallas_call(
+        lambda *refs: rank_space_kernel(
+            *refs,
+            sections=sections,
+            rank=rank,
+            width=width,
+            micro=micro,
+            tokens=tokens,
+            parts=parts,
+        ),
+        out_shape=jax.ShapeDtypeStruct((parts, payload_rows, LANES), jnp.bfloat16),
+        in_specs=[pl.BlockSpec(memory_space=pltpu.MemorySpace.SMEM), vmem] + [hbm] * (sections + 3),
+        out_specs=vmem,
+        scratch_shapes=[
+            pltpu.VMEM((2 * half + 2 * rows, width), jnp.bfloat16),
+            pltpu.VMEM((rank, width), jnp.bfloat16),
+            pltpu.VMEM((half, 2 * half), jnp.float32),
+            pltpu.VMEM((2 * rows, 2 * half), jnp.float32),
+            pltpu.VMEM((sections, rows, half), jnp.float32),
+            pltpu.VMEM((4, half, rows), jnp.float32),
+            pltpu.SemaphoreType.DMA((PIECES, 3 + 2 * sections)),
+        ],
+        compiler_params=pltpu.CompilerParams(vmem_limit_bytes=VMEM_BUDGET),
+        name="rank_space",
+    )(
+        section_index.astype(jnp.int32).reshape(1),
+        masks,
+        entry_tokens.reshape(rows, width),
+        output_gradient.reshape(rows, width),
+        *weights,
+        down,
+    )
+    spread = lax.all_to_all(payload, "dp", 0, 0, tiled=True)
+    summed = pl.pallas_call(
+        sum_kernel,
+        out_shape=jax.ShapeDtypeStruct(payload.shape, jnp.bfloat16),
+        in_specs=[vmem],
+        out_specs=vmem,
+        name="sum_parts",
+    )(spread)
+    gathered = lax.all_to_all(summed, "dp", 0, 0, tiled=True)
+    grad_up, grad_gain = pl.pallas_call(
+        unpack_kernel,
+        out_shape=(
+            jax.ShapeDtypeStruct((rank, width), jnp.float32),
+            jax.ShapeDtypeStruct((1, width), jnp.float32),
+        ),
+        in_specs=[vmem],
+        out_specs=(vmem, vmem),
+        name="unpack",
+    )(gathered)
+    return (grad_up[None], grad_gain)
+
+
+def fits_rank_space(args, sections, parts):
+    micro, tokens, width = args[0].shape[1:]
+    rank = args[2].shape[1]
+    rows = micro * tokens
+    half = -(-sections * rank // LANES) * LANES
+    return (
+        sections & (sections - 1) == 0
+        and width % (parts * LANES) == 0
+        and width % (PIECES * LANES) == 0
+        and rank % 16 == 0
+        and rows % LANES == 0
+        and tokens % 8 == 0
+        and (2 * half + 2 * rows) * width * 2 <= VMEM_BUDGET // 3
+    )
+
+
+def body(*args):
+    if fits_rank_space(args, lax.axis_size("section"), lax.axis_size("dp")):
+        return rank_space_body(*args)
+    return relay_body(*args)
+
+
 def solution(mesh):
     in_specs = (
         P("dp", None, None, None),

time: 369 us -> 119 us (0.32)
  waiting for transfers between devices: 126 us -> 34.4 us
  starting transfers between devices: 65.6 us -> 3.07 us
  other arithmetic: 61.1 us -> 2.33 us
  matrix products: 24 us -> 0 us
  local copies, waits for them, and re-layouts: 23 us -> 0.94 us
  Pallas kernels: 0 us -> 18.8 us
  between operations: 14.1 us -> 0.71 us
  blocking collectives: 51.7 us -> 58.5 us
    ppermute x14 -> x3, starting transfers between devices: 65.5 us -> 3.07 us  [swapped(): return lax.ppermute(block, axis, route)]
    psum x1 -> x0, waiting for transfers between devices: 58.2 us -> none  [body(): summed_up, summed_gain = lax.psum((grad_section, gain_grad), 'dp')]
    all_to_all x0 -> x2, blocking collectives: none -> 53.1 us  [the longest x1 28 us: rank_space_body(): spread = lax.all_to_all(payload, 'dp', 0, 0, tiled=True)]
    psum x2 -> x0, blocking collectives: 51.7 us -> none  [the longest x1 38.7 us: body(): summed_up, summed_gain = lax.psum((grad_section, gain_grad), 'dp')]
    ppermute x14 -> x3, waiting for transfers between devices: 67.5 us -> 34.4 us  [swapped(): return lax.ppermute(block, axis, route)]
    dynamic_update_slice x14 -> x0, other arithmetic: 30 us -> none  [the longest x7 15.5 us: backward_tick(): lax.dynamic_update_index_in_dim(grad_stash, jnp.where(active, branch_grad...]
    dot_general x22 -> x0, matrix products: 24 us -> none  [the longest x7 14.8 us: backward_tick(): jnp.dot(lowrank_gradient, down_rows, preferred_element_type=jnp.float32)]
    pallas_call x0 -> x3, Pallas kernels: none -> 18.8 us  [the longest x1 14.3 us: rank_space_body(): pl.pallas_call(lambda *refs: rank_space_kernel(*refs, sections=sections,...]
  transfers between devices with their start and end apart: 15 -> 3, of which waited for: 15 -> 1; matrix products, arithmetic and copies ran while one was open for 1% -> 1% of each run, Pallas kernels for 0% -> 0%
where the time goes in v1:
time: 119 us
  blocking collectives  58.5 us (49%)
  waiting for transfers between devices  34.4 us (29%)
  Pallas kernels  18.8 us (16%)
  starting transfers between devices  3.07 us (3%)
  other arithmetic  2.33 us (2%)
    ppermute x3, waiting for transfers between devices, swapped(): return lax.ppermute(block, axis, route)  34.4 us
    all_to_all x1, blocking collectives, rank_space_body(): spread = lax.all_to_all(payload, 'dp', 0, 0, tiled=True)  28 us
    all_to_all x1, blocking collectives, rank_space_body(): gathered = lax.all_to_all(summed, 'dp', 0, 0, tiled=True)  25 us
    pallas_call x1, Pallas kernels, rank_space_body(): pl.pallas_call(lambda *refs: rank_space_kernel(*refs, sections=sections,...  14.3 us
    all_gather x1, blocking collectives, rank_space_body(): lax.all_gather(keep[0, 0], 'section').astype(jnp.float32) * valid[None]  5.4 us
    ppermute x3, starting transfers between devices, swapped(): return lax.ppermute(block, axis, route)  3.07 us
    pallas_call x1, Pallas kernels, rank_space_body(): pl.pallas_call(unpack_kernel, out_shape=(jax.ShapeDtypeStruct((rank, widt...  2.41 us
  transfers between devices with their start and end apart: 3, of which 1 were waited for; matrix products, arithmetic and copies ran while one was open for 1% of the time, Pallas kernels for 0%

profile of v1, /device:TPU:0, one launch (start us, length us, event | category | flops | bytes accessed | tf_op | source)
XLA Modules:
  0.0 118.7 jit_solution(9145021831602415477)
XLA Ops:
  0.6 0.0 copy-start.2
  0.6 0.9 mul.27
  1.5 1.3 %multiply_convert_fusion = bf16[48,8192]{1,0:T(8,128)(2,1)S(1)} fusion(f32[8192]{0:T(1024)S(1)} %bitcast.17, bf16[1,48,8192]{2,1,0:T(8,128)(2,1)} %param.9), kind=kLoop, calls=%fused_computation.1 | loop fusion | flops 1179648 | bytes 1605632 | tf_op jit(solution)/shard_map/convert_element_type | solution.py:403
  2.8 0.0 copy-done.2
  2.8 0.0 copy-start.4
  2.8 0.0 copy-start.3
  2.8 0.1 pad_maximum_fusion.refs_4_
  2.9 0.0 copy-start
  2.9 3.1 %collective-permute-start.1 = (bf16[96,8192]{1,0:T(8,128)(2,1)S(1)}, bf16[96,8192]{1,0:T(8,128)(2,1)S(1)}, u32[]{:S(2)}, u32[]{:S(2)}) collective-permute-start(bf16[96,8192]{1,0:T(8,128)(2,1)S(1)} %pad_maximum_fusion.refs_4_), channel_id=1, source_target_pairs={{0,2},{1,3},{2,0},{3,1},{4,6},{5,7},{6,4},{7,5},{8,10},{9,11},{10,... | collective-permute-start | bytes 4718600 | tf_op jit(solution)/shard_map/ppermute | solution.py:165
  6.0 0.0 collective-permute-start
  6.0 34.4 %collective-permute-done.1.refs_6_ = bf16[96,8192]{1,0:T(8,128)(2,1)S(1)} collective-permute-done((bf16[96,8192]{1,0:T(8,128)(2,1)S(1)}, bf16[96,8192]{1,0:T(8,128)(2,1)S(1)}, u32[]{:S(2)}, u32[]{:S(2)}) %collective-permute-start.1) | collective-permute-done | bytes 1572896 | tf_op jit(solution)/shard_map/ppermute | solution.py:165
  40.4 0.0 copy-start.1
  40.4 0.0 collective-permute-start.2
  40.4 0.0 copy-done.4
  40.4 0.1 fusion
  40.5 0.1 reshape.69
  40.6 0.0 copy-done.3
  40.6 5.4 %all-gather = s32[4,1,8,16]{3,2,1,0:T(8,128)S(1)} all-gather(s32[1,1,8,16]{3,2,1,0:T(8,128)S(1)} %copy-done.3), channel_id=2, replica_groups=mesh['dp'=8,'section'=4] {'section'}, dimensions={0}, use_global_device_ids=true | all-gather | bytes 2560 | tf_op jit(solution)/shard_map/all_gather | solution.py:414
  46.0 0.1 reshape.66
  46.1 0.7 copy.11
  46.8 0.0 collective-permute-done.refs_5_
  46.8 0.0 collective-permute-done.2.refs_7_
  46.8 0.0 copy-done
  46.8 0.0 copy-done.1
  46.8 14.3 %rank_space.1 = bf16[8,400,128]{2,1,0:T(8,128)(2,1)} custom-call(s32[1]{0:T(128)} %bitcast.refs_0_, f32[128,5]{1,0:T(8,128)} %bitcast.16, bf16[128,8192]{1,0:T(8,128)(2,1)} %bitcast.13, bf16[128,8192]{1,0:T(8,128)(2,1)} %bitcast.14, bf16[96,8192]{1,0:T(8,128)(2,1)} %copy-done, bf16[96,8192]{1,0:T(8,128)(2,1)} %collective-permute-done.refs_5_, ...), custom_call_target="tpu_custom_call" | custom-call | tf_op jit(solution)/shard_map/rank_space/pallas_call | solution.py:421
  61.1 28.0 %all_to_all.10.parts_ref = bf16[8,400,128]{2,1,0:T(8,128)(2,1)} all-to-all(bf16[8,400,128]{2,1,0:T(8,128)(2,1)} %rank_space.1), channel_id=1, replica_groups=mesh['dp'=8,'section'=4] {'dp'}, dimensions={0} | all-to-all | bytes 1638400 | tf_op jit(solution)/shard_map/all_to_all | solution.py:453
  89.1 2.1 %sum_parts.1 = bf16[8,400,128]{2,1,0:T(8,128)(2,1)} custom-call(bf16[8,400,128]{2,1,0:T(8,128)(2,1)} %all_to_all.10.parts_ref), custom_call_target="tpu_custom_call" | custom-call | tf_op jit(solution)/shard_map/sum_parts/pallas_call | solution.py:454
  91.3 25.0 %all_to_all.11.parts_ref = bf16[8,400,128]{2,1,0:T(8,128)(2,1)} all-to-all(bf16[8,400,128]{2,1,0:T(8,128)(2,1)} %sum_parts.1), channel_id=1, replica_groups=mesh['dp'=8,'section'=4] {'dp'}, dimensions={0} | all-to-all | bytes 1638400 | tf_op jit(solution)/shard_map/all_to_all | solution.py:461
  116.3 2.4 %unpack.1 = (f32[48,8192]{1,0:T(8,128)}, f32[1,8192]{1,0:T(1,128)}) custom-call(bf16[8,400,128]{2,1,0:T(8,128)(2,1)} %all_to_all.11.parts_ref), custom_call_target="tpu_custom_call" | custom-call | tf_op jit(solution)/shard_map/unpack/pallas_call | solution.py:462
  (2 shorter events, 0.0 us)
Async XLA Ops:
  0.6 2.1 %copy-start.2 = (bf16[1,48,8192]{2,1,0:T(8,128)(2,1)S(1)}, bf16[1,48,8192]{2,1,0:T(8,128)(2,1)}, u32[]{:S(2)}) copy-start(bf16[1,48,8192]{2,1,0:T(8,128)(2,1)} %param.10) | copy-start | bytes 2359300
  2.8 37.6 %copy-start.4 = (s32[1,8]{1,0:T(1,128)S(1)}, s32[1,8]{1,0:T(1,128)}, u32[]{:S(2)}) copy-start(s32[1,8]{1,0:T(1,128)} %param.12) | copy-start | bytes 100
  2.8 37.8 %copy-start.3 = (s32[1,1,8,16]{3,2,1,0:T(8,128)S(1)}, s32[1,1,8,16]{3,2,1,0:T(8,128)}, u32[]{:S(2)}) copy-start(s32[1,1,8,16]{3,2,1,0:T(8,128)} %param.13) | copy-start | bytes 1540
  2.9 43.9 %copy-start = (bf16[96,8192]{1,0:T(8,128)(2,1)}, bf16[96,8192]{1,0:T(8,128)(2,1)S(1)}, u32[]{:S(2)}) copy-start(bf16[96,8192]{1,0:T(8,128)(2,1)S(1)} %pad_maximum_fusion.refs_4_) | copy-start | bytes 4718596
  2.9 37.5 %collective-permute-start.1 = (bf16[96,8192]{1,0:T(8,128)(2,1)S(1)}, bf16[96,8192]{1,0:T(8,128)(2,1)S(1)}, u32[]{:S(2)}, u32[]{:S(2)}) collective-permute-start(bf16[96,8192]{1,0:T(8,128)(2,1)S(1)} %pad_maximum_fusion.refs_4_), channel_id=1, source_target_pairs={{0,2},{1,3},{2,0},{3,1},{4,6},{5,7},{6,4},{7,5},{8,10},{9,11},{10,... | collective-permute-start | bytes 4718600 | tf_op jit(solution)/shard_map/ppermute | solution.py:165
  6.0 40.8 %collective-permute-start = (bf16[96,8192]{1,0:T(8,128)(2,1)S(1)}, bf16[96,8192]{1,0:T(8,128)(2,1)}, u32[]{:S(2)}, u32[]{:S(2)}) collective-permute-start(bf16[96,8192]{1,0:T(8,128)(2,1)S(1)} %pad_maximum_fusion.refs_4_), channel_id=1, source_target_pairs={{0,1},{1,0},{2,3},{3,2},{4,5},{5,4},{6,7},{7,6},{8,9},{9,8},{10,11... | collective-permute-start | bytes 4718600 | tf_op jit(solution)/shard_map/ppermute | solution.py:165
  40.4 6.4 %copy-start.1 = (bf16[96,8192]{1,0:T(8,128)(2,1)}, bf16[96,8192]{1,0:T(8,128)(2,1)S(1)}, u32[]{:S(2)}) copy-start(bf16[96,8192]{1,0:T(8,128)(2,1)S(1)} %collective-permute-done.1.refs_6_) | copy-start | bytes 4718596
  40.4 6.4 %collective-permute-start.2 = (bf16[96,8192]{1,0:T(8,128)(2,1)S(1)}, bf16[96,8192]{1,0:T(8,128)(2,1)}, u32[]{:S(2)}, u32[]{:S(2)}) collective-permute-start(bf16[96,8192]{1,0:T(8,128)(2,1)S(1)} %collective-permute-done.1.refs_6_), channel_id=1, source_target_pairs={{0,1},{1,0},{2,3},{3,2},{4,5},{5,4},{6,7},{7,6},{8,9},{9,8},{10,11... | collective-permute-start | bytes 4718600 | tf_op jit(solution)/shard_map/ppermute | solution.py:165
